TPU v7x, 32 devices: a whole 2x2x4 slice. The times are simulated.
32 devices in a mesh: texel: 8 (over y, x, core), light: 4 (over z).
Axes of the slice: x: 2, y: 2, z: 4, core: 2. Of those that a mesh axis runs over, the one named last changes fastest.
Arguments:
- tex_feat: bfloat16 [8192, 512], P('texel'), may hold values from -18 to 18
- light_feat: bfloat16 [6144, 512], P('light'), may hold values from -0.25 to 0.25
- sketch: bfloat16 [6144, 256], P('light'), may hold values from -0.078125 to 0.078125
- row_counts: int32 [8], replicated, may hold values from 1 to 1024, 4096 in all
Outputs:
- basis: float32 [8192, 256], P('texel')
- coeffs: float32 [256, 6144], P('texel', 'light')
Inputs may be any that keep to these rules, and one draw needn't show every extreme that they name: row_counts sums to 8 * 512; some entry equals 1024.
All inputs are finite; a program needn't handle non-finite values.
Results may differ from a plain program's by a relative error of at most 0.0034.
Values sent between devices are 32-bit elements; how exact they have to be, the bound alone decides.
A program may use at most 64 MiB of HBM per device.

v0:
```python
import jax
import jax.numpy as jnp
from jax import lax
from jax.sharding import PartitionSpec as P


def on_device(tex_feat, light_feat, sketch, row_counts):
    capacity = tex_feat.shape[0]
    own_count = row_counts[lax.axis_index("texel")]
    valid_total = jnp.sum(row_counts).astype(jnp.float32)
    logits = lax.dot_general(
        tex_feat, light_feat, (((1,), (1,)), ((), ())), preferred_element_type=jnp.float32
    )
    tile_block = jnp.sin(logits).astype(jnp.bfloat16)
    row_valid = (lax.iota(jnp.int32, capacity) < own_count).astype(jnp.float32)
    partial_value = (
        jnp.dot(tile_block, sketch, preferred_element_type=jnp.float32) * row_valid[:, None]
    )
    sketched = lax.psum(partial_value, "light")
    gram_local = jnp.dot(sketched.T, sketched, precision=lax.Precision.HIGHEST)
    gram_matrix = lax.psum(gram_local, "texel") / valid_total
    factor = jnp.linalg.cholesky(gram_matrix)
    basis = jax.scipy.linalg.solve_triangular(factor, sketched.T, lower=True).T
    basis_half = basis.astype(jnp.bfloat16)
    coeffs = lax.psum_scatter(
        lax.dot_general(
            basis_half, tile_block, (((0,), (0,)), ((), ())), preferred_element_type=jnp.float32
        ),
        "texel",
        scatter_dimension=0,
        tiled=True,
    ) / jnp.sqrt(valid_total)
    return (basis, coeffs)


def solution(mesh):
    placed = (P("texel", None), P("light", None), P("light", None), P())
    return jax.shard_map(
        on_device,
        mesh=mesh,
        in_specs=placed,
        out_specs=(P("texel", None), P("texel", "light")),
        check_vma=False,
    )
```

profile of v0, /device:TPU:0, one launch (start us, length us, event | category | flops | bytes accessed | tf_op | source)
XLA Modules:
  0.0 261.9 jit_solution(2642677506085759507)
XLA Ops:
  7.2 0.0 copy-start
  7.2 0.0 all-reduce.4.cloned.1.call-start
  7.2 1.3 dynamic_slice.3
  8.6 0.6 fusion.10
  9.2 0.0 copy-done
  9.2 0.0 copy-start.4
  9.3 23.0 %sine_convert_fusion = bf16[1024,1536]{1,0:T(8,128)(2,1)S(1)} fusion(bf16[1024,512]{1,0:T(8,128)(2,1)} %param.4, bf16[1536,512]{1,0:T(8,128)(2,1)S(1)} %copy-done), kind=kOutput, calls=%fused_computation.2 | convolution fusion | flops 1612185600 | bytes 5767168 | tf_op jit(solution)/shard_map/dot_general | solution.py:11
  32.2 0.0 copy-start.2
  32.2 1.7 copy-done.2
  33.9 0.0 copy-done.4
  33.9 1.9 convolution_multiply_fusion
  35.8 0.0 all-reduce.4.cloned.1.call-update
  35.9 0.0 all-reduce.6.cloned.1.call-start
  35.9 54.7 %all-reduce.4.cloned.1.call-done = f32[1024,256]{1,0:T(8,128)} async-done(((f32[1024,256]{1,0:T(8,128)}), f32[1024,256]{1,0:T(8,128)}) %all-reduce.4.cloned.1.call-update) | async-done | bytes 1048592 | tf_op jit(solution)/shard_map/psum | solution.py:19
  90.6 4.1 %fusion.12 = f32[256,256]{0,1:T(8,128)} fusion(f32[1024,256]{1,0:T(8,128)} %all-reduce.4.cloned.1.call-done), kind=kOutput, calls=%fused_computation.37 | convolution fusion | flops 805306368 | bytes 1310720 | tf_op jit(solution)/shard_map/dot_general | solution.py:20
  94.8 0.0 all-reduce.6.cloned.1.call-update
  94.8 0.2 reduce-scatter.2.cloned.1.call-start
  95.0 0.0 copy-done.6
  95.1 0.6 reduce_sum.9
  96.3 51.8 %all-reduce.6.cloned.1.call-done = f32[256,256]{0,1:T(8,128)} async-done(((f32[256,256]{0,1:T(8,128)}), f32[256,256]{0,1:T(8,128)}) %all-reduce.6.cloned.1.call-update) | async-done | bytes 262160 | tf_op jit(solution)/shard_map/psum | solution.py:21
  148.1 1.0 broadcast_divide_fusion
  149.1 0.1 copy.7
  149.2 1.0 fusion.4
  150.2 11.7 %cholesky.50 = f32[128,128]{1,0:T(8,128)S(1)} custom-call(f32[128,128]{1,0:T(8,128)S(1)} %cholesky.118), custom_call_target="Cholesky" | custom-call | tf_op jit(solution)/shard_map/jit(cholesky)/cholesky | solution.py:22
  162.0 9.8 %custom-call.15 = f32[1,128,128]{1,2,0:T(8,128)S(1)} custom-call(f32[1,128,128]{2,1,0:T(8,128)S(1)} %get-tuple-element.25), custom_call_target="InvertDiagBlocksLowerTriangular" | custom-call | tf_op jit(solution)/shard_map/jit(cholesky)/cholesky | solution.py:22
  171.8 0.2 constant_dynamic-update-slice_fusion.1
  172.0 0.3 convolution_subtract_fusion.1
  172.3 11.7 %cholesky.105 = f32[128,128]{1,0:T(8,128)S(1)} custom-call(f32[128,128]{1,0:T(8,128)S(1)} %convolution_subtract_fusion.1), custom_call_target="Cholesky" | custom-call | tf_op jit(solution)/shard_map/jit(cholesky)/cholesky | solution.py:22
  184.1 0.7 compare_reduce_fusion
  186.0 0.1 triangular_solve.57
  186.1 4.1 %while.1 = (s32[]{:T(128)}, f32[256,256]{1,0:T(8,128)S(1)}, s32[2,2]{1,0:T(2,128)S(1)}, f32[2,128,128]{2,1,0:T(8,128)S(1)}, s32[]{:T(128)}) while((s32[]{:T(128)}, f32[256,256]{1,0:T(8,128)S(1)}, s32[2,2]{1,0:T(2,128)S(1)}, f32[2,128,128]{2,1,0:T(8,128)S(1)}, s32[]{:T(128)}) %tuple.28), condition=%wide.while_cond, body=%wide.while_body.sunk | while | flops 2 | bytes 131189 | solution.py:23
  186.3 0.6 fusion.25
  186.9 1.4 bitcast_dynamic-update-slice_fusion.2
  188.3 0.6 fusion.25
  188.8 1.4 bitcast_dynamic-update-slice_fusion.2
  190.2 0.0 copy-start.5
  190.2 0.6 copy-done.5
  190.9 20.5 %custom-call.16 = f32[2,128,128]{1,2,0:T(8,128)S(1)} custom-call(f32[2,128,128]{2,1,0:T(8,128)} %copy-done.5), custom_call_target="InvertDiagBlocksLowerTriangular" | custom-call | tf_op jit(solution)/shard_map/jit(_solve_triangular)/triangular_solve | solution.py:23
  211.4 0.0 copy-start.3
  211.4 0.6 fusion
  212.0 1.0 convolution_subtract_fusion
  213.0 0.6 fusion.6
  213.7 2.2 fusion.2
  215.9 0.0 reduce-scatter.2.cloned.1.call-update
  215.9 1.1 maximum_bitcast_fusion
  217.0 2.5 copy.8
  219.5 34.2 %reduce-scatter.2.cloned.1.call-done = f32[32,1536]{1,0:T(8,128)} async-done(((f32[256,1536]{1,0:T(8,128)}), f32[32,1536]{1,0:T(8,128)}) %reduce-scatter.2.cloned.1.call-update) | async-done | bytes 196624 | tf_op jit(solution)/shard_map/reduce_scatter | solution.py:25
  253.7 1.6 broadcast_divide_fusion.1
  (13 shorter events, 0.2 us)
Async XLA Ops:
  7.2 2.1 copy-start
  7.2 83.5 %all-reduce.4.cloned.1.call-start = ((), (), s32[]{:S(2)}) async-start(), calls=%async_computation.1 | async-start | bytes 2097152 | tf_op jit(solution)/shard_map/psum | solution.py:19
  9.2 24.7 %copy-start.4 = (bf16[1536,256]{1,0:T(8,128)(2,1)S(1)}, bf16[1536,256]{1,0:T(8,128)(2,1)}, u32[]{:S(2)}) copy-start(bf16[1536,256]{1,0:T(8,128)(2,1)} %param.6) | copy-start | bytes 2359300
  32.2 1.7 copy-start.2
  35.8 59.2 %copy-start.6 = (s32[8]{0:T(128)S(1)}, s32[8]{0:T(128)}, u32[]{:S(2)}) copy-start(s32[8]{0:T(128)} %param.7) | copy-start | bytes 100
  35.9 112.3 %all-reduce.6.cloned.1.call-start = ((), (), s32[]{:S(2)}) async-start(), calls=%async_computation.2 | async-start | bytes 524288 | tf_op jit(solution)/shard_map/psum | solution.py:21
  90.6 120.7 %copy-start.1 = (f32[1024,256]{1,0:T(8,128)S(1)}, f32[1024,256]{1,0:T(8,128)}, u32[]{:S(2)}) copy-start(f32[1024,256]{1,0:T(8,128)} %all-reduce.4.cloned.1.call-done) | copy-start | bytes 3145732
  94.8 158.9 %reduce-scatter.2.cloned.1.call-start = ((), (), s32[]{:S(2)}) async-start(), calls=%async_computation.3 | async-start | bytes 1769472 | tf_op jit(solution)/shard_map/reduce_scatter | solution.py:25
  190.2 0.7 copy-start.5
  211.4 2.3 copy-start.3
Sparse Core Ops, SparseCore 0:
  36.0 54.6 all-reduce.3
  94.9 53.1 all-reduce.5
  216.0 37.6 reduce-scatter.1
where the time goes:
time: 262 us
  waiting for transfers between devices  141 us (54%)
  other arithmetic  60.4 us (23%)
  matrix products  34 us (13%)
  between operations  15.8 us (6%)
  local copies, waits for them, and re-layouts  10.3 us (4%)
    psum x1, waiting for transfers between devices, on_device(): sketched = lax.psum(partial_value, 'light')  54.7 us
    psum x1, waiting for transfers between devices, on_device(): gram_matrix = lax.psum(gram_local, 'texel') / valid_total  51.8 us
    reduce_scatter x1, waiting for transfers between devices, on_device(): lax.psum_scatter(lax.dot_general(basis_half, tile_block, (((0,), (0,)), (...  34.2 us
    another operation x6, other arithmetic, on_device(): factor = jnp.linalg.cholesky(gram_matrix)  34 us
    dot_general x1, matrix products, on_device(): lax.dot_general(tex_feat, light_feat, (((1,), (1,)), ((), ())), preferred...  23 us
    another operation x3, other arithmetic, on_device(): basis = jax.scipy.linalg.solve_triangular(factor, sketched.T, lower=True).T  20.5 us
  transfers between devices with their start and end apart: 3, of which 3 were waited for; matrix products, arithmetic and copies ran while one was open for 2% of the time, Pallas kernels for 0%

commit v1 on v0

--- a/solution.py
+++ b/solution.py
@@ -16,7 +16,7 @@
     partial_value = (
         jnp.dot(tile_block, sketch, preferred_element_type=jnp.float32) * row_valid[:, None]
     )
-    sketched = lax.psum(partial_value, "light")
+    sketched = jnp.sum(lax.all_gather(partial_value, "light"), axis=0)
     gram_local = jnp.dot(sketched.T, sketched, precision=lax.Precision.HIGHEST)
     gram_matrix = lax.psum(gram_local, "texel") / valid_total
     factor = jnp.linalg.cholesky(gram_matrix)

time: 262 us -> 292 us (1.11)
  waiting for transfers between devices: 141 us -> 169 us
    all_gather x0 -> x1, waiting for transfers between devices: none -> 83.6 us  [on_device(): sketched = jnp.sum(lax.all_gather(partial_value, 'light'), axis=0)]
    psum x1 -> x0, waiting for transfers between devices: 54.7 us -> none  [on_device(): sketched = lax.psum(partial_value, 'light')]
  transfers between devices with their start and end apart: 3 -> 3, of which waited for: 3 -> 3; matrix products, arithmetic and copies ran while one was open for 2% -> 1% of each run, Pallas kernels for 0% -> 0%
where the time goes in v1:
time: 292 us; the launch traced here: 291 us
  waiting for transfers between devices  169 us (58%)
  other arithmetic  63.1 us (22%)
  matrix products  32.3 us (11%)
  between operations  15.9 us (5%)
  local copies, waits for them, and re-layouts  10.5 us (4%)
    all_gather x1, waiting for transfers between devices, on_device(): sketched = jnp.sum(lax.all_gather(partial_value, 'light'), axis=0)  83.6 us
    psum x1, waiting for transfers between devices, on_device(): gram_matrix = lax.psum(gram_local, 'texel') / valid_total  50.9 us
    reduce_scatter x1, waiting for transfers between devices, on_device(): lax.psum_scatter(lax.dot_general(basis_half, tile_block, (((0,), (0,)), (...  34.3 us
    another operation x6, other arithmetic, on_device(): factor = jnp.linalg.cholesky(gram_matrix)  34 us
    dot_general x1, matrix products, on_device(): lax.dot_general(tex_feat, light_feat, (((1,), (1,)), ((), ())), preferred...  23 us
    another operation x3, other arithmetic, on_device(): basis = jax.scipy.linalg.solve_triangular(factor, sketched.T, lower=True).T  20.5 us
  transfers between devices with their start and end apart: 3, of which 3 were waited for; matrix products, arithmetic and copies ran while one was open for 1% of the time, Pallas kernels for 0%

profile of v1, /device:TPU:0, one launch (start us, length us, event | category | flops | bytes accessed | tf_op | source)
XLA Modules:
  0.0 291.3 jit_solution(13809831102737779570)
XLA Ops:
  7.2 0.0 copy-start
  7.2 0.0 all-gather.3.cloned.1.call-start
  7.2 1.3 dynamic_slice.3
  8.6 0.6 fusion.10
  9.2 0.0 copy-done
  9.2 0.0 copy-start.3
  9.3 23.0 %sine_convert_fusion = bf16[1024,1536]{1,0:T(8,128)(2,1)S(1)} fusion(bf16[1024,512]{1,0:T(8,128)(2,1)} %param.4, bf16[1536,512]{1,0:T(8,128)(2,1)S(1)} %copy-done), kind=kOutput, calls=%fused_computation.2 | convolution fusion | flops 1612185600 | bytes 5767168 | tf_op jit(solution)/shard_map/dot_general | solution.py:11
  32.2 0.0 copy-start.1
  32.2 1.7 copy-done.1
  33.9 0.0 copy-done.3
  33.9 1.9 convolution_multiply_fusion
  35.9 0.0 all-gather.3.cloned.1.call-update
  35.9 0.0 all-reduce.3.cloned.1.call-start
  35.9 83.6 %all-gather.3.cloned.1.call-done = f32[4096,256]{1,0:T(8,128)} async-done(((f32[1024,256]{1,0:T(8,128)}), f32[4096,256]{1,0:T(8,128)}) %all-gather.3.cloned.1.call-update) | async-done | bytes 4194320 | tf_op jit(solution)/shard_map/all_gather | solution.py:19
  119.5 2.6 reduce_sum.18
  122.1 2.5 fusion.12
  124.6 0.0 all-reduce.3.cloned.1.call-update
  124.7 0.2 reduce-scatter.2.cloned.1.call-start
  124.9 0.0 copy-done.5
  124.9 0.7 reduce_sum.19
  126.2 50.9 %all-reduce.3.cloned.1.call-done = f32[256,256]{0,1:T(8,128)} async-done(((f32[256,256]{0,1:T(8,128)}), f32[256,256]{0,1:T(8,128)}) %all-reduce.3.cloned.1.call-update) | async-done | bytes 262160 | tf_op jit(solution)/shard_map/psum | solution.py:21
  177.2 1.0 broadcast_divide_fusion
  178.2 0.1 copy.7
  178.3 1.0 fusion.4
  179.3 11.7 %cholesky.50 = f32[128,128]{1,0:T(8,128)S(1)} custom-call(f32[128,128]{1,0:T(8,128)S(1)} %cholesky.118), custom_call_target="Cholesky" | custom-call | tf_op jit(solution)/shard_map/jit(cholesky)/cholesky | solution.py:22
  191.1 9.8 %custom-call.15 = f32[1,128,128]{1,2,0:T(8,128)S(1)} custom-call(f32[1,128,128]{2,1,0:T(8,128)S(1)} %get-tuple-element.25), custom_call_target="InvertDiagBlocksLowerTriangular" | custom-call | tf_op jit(solution)/shard_map/jit(cholesky)/cholesky | solution.py:22
  200.9 0.2 constant_dynamic-update-slice_fusion.1
  201.1 0.3 convolution_subtract_fusion.1
  201.4 11.7 %cholesky.105 = f32[128,128]{1,0:T(8,128)S(1)} custom-call(f32[128,128]{1,0:T(8,128)S(1)} %convolution_subtract_fusion.1), custom_call_target="Cholesky" | custom-call | tf_op jit(solution)/shard_map/jit(cholesky)/cholesky | solution.py:22
  213.1 0.7 compare_reduce_fusion
  215.2 0.1 triangular_solve.57
  215.3 4.3 %while.1 = (s32[]{:T(128)}, f32[256,256]{1,0:T(8,128)S(1)}, s32[2,2]{1,0:T(2,128)S(1)}, f32[2,128,128]{2,1,0:T(8,128)S(1)}, s32[]{:T(128)}) while((s32[]{:T(128)}, f32[256,256]{1,0:T(8,128)S(1)}, s32[2,2]{1,0:T(2,128)S(1)}, f32[2,128,128]{2,1,0:T(8,128)S(1)}, s32[]{:T(128)}) %tuple.28), condition=%wide.while_cond, body=%wide.while_body.sunk | while | flops 2 | bytes 131181 | solution.py:23
  215.5 0.6 fusion.25
  216.1 1.4 bitcast_dynamic-update-slice_fusion.2
  217.5 0.6 fusion.25
  218.1 1.4 bitcast_dynamic-update-slice_fusion.2
  219.6 0.0 copy-start.4
  219.6 0.6 copy-done.4
  220.2 20.5 %custom-call.16 = f32[2,128,128]{1,2,0:T(8,128)S(1)} custom-call(f32[2,128,128]{2,1,0:T(8,128)} %copy-done.4), custom_call_target="InvertDiagBlocksLowerTriangular" | custom-call | tf_op jit(solution)/shard_map/jit(_solve_triangular)/triangular_solve | solution.py:23
  240.7 0.6 fusion
  241.4 1.0 convolution_subtract_fusion
  242.4 0.6 fusion.6
  243.0 2.2 fusion.2
  245.2 0.0 reduce-scatter.2.cloned.1.call-update
  245.3 1.0 maximum_bitcast_fusion
  246.3 2.5 copy.8
  248.8 34.3 %reduce-scatter.2.cloned.1.call-done = f32[32,1536]{1,0:T(8,128)} async-done(((f32[256,1536]{1,0:T(8,128)}), f32[32,1536]{1,0:T(8,128)}) %reduce-scatter.2.cloned.1.call-update) | async-done | bytes 196624 | tf_op jit(solution)/shard_map/reduce_scatter | solution.py:25
  283.1 1.6 broadcast_divide_fusion.1
  (12 shorter events, 0.2 us)
Async XLA Ops:
  7.2 2.1 copy-start
  7.2 112.3 %all-gather.3.cloned.1.call-start = ((), (), s32[]{:S(2)}) async-start(), calls=%async_computation.3 | async-start | bytes 5242880 | tf_op jit(solution)/shard_map/all_gather | solution.py:19
  9.2 24.7 %copy-start.3 = (bf16[1536,256]{1,0:T(8,128)(2,1)S(1)}, bf16[1536,256]{1,0:T(8,128)(2,1)}, u32[]{:S(2)}) copy-start(bf16[1536,256]{1,0:T(8,128)(2,1)} %param.6) | copy-start | bytes 2359300
  32.2 1.7 copy-start.1
  35.9 141.3 %all-reduce.3.cloned.1.call-start = ((), (), s32[]{:S(2)}) async-start(), calls=%async_computation.1 | async-start | bytes 524288 | tf_op jit(solution)/shard_map/psum | solution.py:21
  119.5 5.4 %copy-start.5 = (s32[8]{0:T(128)S(1)}, s32[8]{0:T(128)}, u32[]{:S(2)}) copy-start(s32[8]{0:T(128)} %param.7) | copy-start | bytes 100
  124.7 158.5 %reduce-scatter.2.cloned.1.call-start = ((), (), s32[]{:S(2)}) async-start(), calls=%async_computation.2 | async-start | bytes 1769472 | tf_op jit(solution)/shard_map/reduce_scatter | solution.py:25
  219.6 0.7 copy-start.4
  240.7 2.3 copy-start.2
Sparse Core Ops, SparseCore 0:
  36.0 83.4 all-gather.2
  124.8 52.3 all-reduce.2
  245.4 37.7 reduce-scatter.1
